TPU v7x, 32 devices: a whole 2x2x4 slice. The times are simulated.
32 devices in a mesh: bar: 16 (over z, x, core), lat: 2 (over y).
Axes of the slice: x: 2, y: 2, z: 4, core: 2. Of those that a mesh axis runs over, the one named last changes fastest.
Arguments:
- displace: float32 [3, 96, 16, 128], P(None, 'bar', 'lat'), may hold values from -6 to 6
- velocity: float32 [3, 96, 16, 128], P(None, 'bar', 'lat'), may hold values from -6 to 6
- bond_low: int32 [96, 16, 128], P('bar', 'lat'), may hold values from 0 to 2147483646
- bond_high: int32 [96, 16, 128], P('bar', 'lat'), may hold values from 0 to 1073741823
- bc_type: int32 [16], replicated, may hold values from 0 to 3
Outputs:
- displace_out: float32 [3, 96, 16, 128], P(None, 'bar', 'lat')
- velocity_out: float32 [3, 96, 16, 128], P(None, 'bar', 'lat')
All inputs are finite; a program needn't handle non-finite values.
Results may differ from a plain program's by a relative error of at most 0.00002.
Values sent between devices are 32-bit elements; how exact they have to be, the bound alone decides.
A program may use at most 64 MiB of HBM per device.

v0:
```python
import jax
import jax.numpy as jnp
from jax import lax
from jax.sharding import PartitionSpec as P

STEPS = 2


modulus = 0.1
time_step = 0.5


def with_halo(cells, sides, width):
    for axis, dim in sides:
        count = lax.axis_size(axis)
        ends = count - 1
        head = lax.slice_in_dim(cells, 0, width, axis=dim)
        tail = lax.slice_in_dim(cells, cells.shape[dim] - width, cells.shape[dim], axis=dim)
        cells = jnp.concatenate(
            [
                lax.ppermute(tail, axis, [(i, (i + 1) % count) for i in range(ends)]),
                cells,
                lax.ppermute(head, axis, [((i + 1) % count, i) for i in range(ends)]),
            ],
            axis=dim,
        )
    return cells


def bond_offsets():
    found = []
    for off_x in range(-3, 4):
        for off_y in range(-3, 4):
            for off_z in range(-3, 4):
                square = off_x * off_x + off_y * off_y + off_z * off_z
                if square == 0 or square > 9:
                    continue
                if (
                    off_x > 0
                    or (off_x == 0 and off_y > 0)
                    or (off_x == 0 and off_y == 0 and (off_z > 0))
                ):
                    found.append((off_x, off_y, off_z))
    return found


def inside(coords, shift_by, total):
    moved = coords + shift_by
    return ((moved >= 0) & (moved < total)).astype(jnp.float32)


def bond_forces(moving, low_bits, high_bits, anchor_x, anchor_y, total_x, total_y):
    size_x, size_y, size_z = (moving.shape[1], moving.shape[2], moving.shape[3])
    padded = jnp.pad(moving, ((0, 0), (3, 3), (3, 3), (3, 3)))
    coord_x = anchor_x + jnp.arange(size_x, dtype=jnp.int32)
    coord_y = anchor_y + jnp.arange(size_y, dtype=jnp.int32)
    coord_z = jnp.arange(size_z, dtype=jnp.int32)
    here_x = inside(coord_x, 0, total_x)
    here_y = inside(coord_y, 0, total_y)
    force_x = jnp.zeros(moving.shape[1:], jnp.float32)
    force_y = jnp.zeros(moving.shape[1:], jnp.float32)
    force_z = jnp.zeros(moving.shape[1:], jnp.float32)
    for number, (off_x, off_y, off_z) in enumerate(bond_offsets()):
        if number < 31:
            flag_word, bit_pos = (low_bits, number)
        else:
            flag_word, bit_pos = (high_bits, number - 31)
        intact = (1 - jnp.bitwise_and(jnp.right_shift(flag_word, bit_pos), 1)).astype(jnp.float32)
        neighbour = padded[
            :,
            3 + off_x : 3 + off_x + size_x,
            3 + off_y : 3 + off_y + size_y,
            3 + off_z : 3 + off_z + size_z,
        ]
        mask_x = here_x * inside(coord_x, off_x, total_x)
        mask_y = here_y * inside(coord_y, off_y, total_y)
        mask_z = inside(coord_z, off_z, size_z)
        reach_mask = mask_x[:, None, None] * mask_y[None, :, None] * mask_z[None, None, :]
        stretch = (
            off_x * (neighbour[0] - moving[0])
            + off_y * (neighbour[1] - moving[1])
            + off_z * (neighbour[2] - moving[2])
        )
        length = float(off_x * off_x + off_y * off_y + off_z * off_z) ** 1.5
        bond_term = modulus / length * intact * reach_mask * stretch
        bond_pad = jnp.pad(bond_term, 3)
        back_term = bond_pad[
            3 - off_x : 3 - off_x + size_x,
            3 - off_y : 3 - off_y + size_y,
            3 - off_z : 3 - off_z + size_z,
        ]
        net_term = bond_term - back_term
        force_x = force_x + off_x * net_term
        force_y = force_y + off_y * net_term
        force_z = force_z + off_z * net_term
    return jnp.stack([force_x, force_y, force_z])


def plane_retain(bc_type, first_plane, count, per_slab):
    planes = first_plane + jnp.arange(count, dtype=jnp.int32)
    slabs = jnp.arange(bc_type.shape[0], dtype=jnp.int32)
    match = (planes[:, None] // per_slab == slabs[None, :]).astype(jnp.float32)
    code = jnp.sum(match * bc_type.astype(jnp.float32)[None, :], axis=1)
    return (1.0 - 0.2 * code)[None, :, None, None]


def local(displace, velocity, bond_low, bond_high, bc_type):
    size_x, size_y = (displace.shape[1], displace.shape[2])
    total_x = size_x * lax.axis_size("bar")
    total_y = size_y * lax.axis_size("lat")
    start_x = lax.axis_index("bar") * size_x
    start_y = lax.axis_index("lat") * size_y
    packed = jnp.stack([bond_low, bond_high])
    rims = with_halo(packed, (("bar", 1), ("lat", 2)), 3)
    retain = plane_retain(bc_type, start_x, size_x, size_x)
    for step_no in range(STEPS):
        wide = with_halo(displace, (("bar", 1), ("lat", 2)), 3)
        forces = bond_forces(wide, rims[0], rims[1], start_x - 3, start_y - 3, total_x, total_y)
        forces = forces[:, 3:-3, 3:-3, :]
        velocity = retain * (velocity + time_step * forces)
        displace = displace + time_step * velocity
    return (displace, velocity)


def solution(mesh):
    return jax.shard_map(
        local,
        mesh=mesh,
        in_specs=(
            P(None, "bar", "lat", None),
            P(None, "bar", "lat", None),
            P("bar", "lat", None),
            P("bar", "lat", None),
            P(),
        ),
        out_specs=(P(None, "bar", "lat", None), P(None, "bar", "lat", None)),
        check_vma=False,
    )
```

profile of v0, /device:TPU:12, one launch (start us, length us, event | category | flops | bytes accessed | tf_op | source)
XLA Modules:
  0.0 67.4 jit_solution(7043995345013164687)
XLA Ops:
  0.7 0.8 %fusion.993 = (f32[3,3,8,128]{3,2,1,0:T(8,128)S(1)}, f32[3,3,8,128]{3,2,1,0:T(8,128)S(1)}) fusion(f32[3,6,8,128]{3,2,1,0:T(8,128)} %param.5), kind=kLoop, calls=%fused_computation.1726 | loop fusion | bytes 147456 | tf_op jit(solution)/shard_map/slice | solution.py:17
  1.5 1.9 %collective-permute-start.4 = (f32[3,3,8,128]{3,2,1,0:T(8,128)S(1)}, f32[3,3,8,128]{3,2,1,0:T(8,128)S(1)}, u32[]{:S(2)}, u32[]{:S(2)}) collective-permute-start(f32[3,3,8,128]{3,2,1,0:T(8,128)S(1)} %get-tuple-element.141), channel_id=1, source_target_pairs={{0,2},{2,4},{4,6},{6,8},{8,10},{10,12},{12,14},{14,16},{16,18},{18... | collective-permute-start | bytes 110600 | tf_op jit(solution)/shard_map/ppermute | solution.py:21
  3.4 4.5 %collective-permute-start.5 = (f32[3,3,8,128]{3,2,1,0:T(8,128)S(1)}, f32[3,3,8,128]{3,2,1,0:T(8,128)S(1)}, u32[]{:S(2)}, u32[]{:S(2)}) collective-permute-start(f32[3,3,8,128]{3,2,1,0:T(8,128)S(1)} %get-tuple-element.140), channel_id=1, source_target_pairs={{2,0},{4,2},{6,4},{8,6},{10,8},{12,10},{14,12},{16,14},{18,16},{20... | collective-permute-start | bytes 110600 | tf_op jit(solution)/shard_map/ppermute | solution.py:23
  7.9 0.8 %fusion.986 = (s32[2,3,8,128]{3,2,1,0:T(8,128)S(1)}, s32[2,3,8,128]{3,2,1,0:T(8,128)S(1)}) fusion(s32[1,6,8,128]{3,2,1,0:T(8,128)} %bitcast.624, s32[1,6,8,128]{3,2,1,0:T(8,128)} %bitcast.627), kind=kLoop, calls=%fused_computation.1678 | loop fusion | flops 12288 | bytes 98304 | tf_op jit(solution)/shard_map/stack | solution.py:113
  8.7 1.9 %collective-permute-start.1 = (s32[2,3,8,128]{3,2,1,0:T(8,128)S(1)}, s32[2,3,8,128]{3,2,1,0:T(8,128)S(1)}, u32[]{:S(2)}, u32[]{:S(2)}) collective-permute-start(s32[2,3,8,128]{3,2,1,0:T(8,128)S(1)} %get-tuple-element.143), channel_id=1, source_target_pairs={{2,0},{4,2},{6,4},{8,6},{10,8},{12,10},{14,12},{16,14},{18,16},{20... | collective-permute-start | bytes 73736 | tf_op jit(solution)/shard_map/ppermute | solution.py:23
  10.6 2.4 %collective-permute-start = (s32[2,3,8,128]{3,2,1,0:T(8,128)S(1)}, s32[2,3,8,128]{3,2,1,0:T(8,128)S(1)}, u32[]{:S(2)}, u32[]{:S(2)}) collective-permute-start(s32[2,3,8,128]{3,2,1,0:T(8,128)S(1)} %get-tuple-element.142), channel_id=1, source_target_pairs={{0,2},{2,4},{4,6},{6,8},{8,10},{10,12},{12,14},{14,16},{16,18},{18... | collective-permute-start | bytes 73736 | tf_op jit(solution)/shard_map/ppermute | solution.py:21
  14.1 2.5 %collective-permute-done = s32[2,3,8,128]{3,2,1,0:T(8,128)S(1)} collective-permute-done((s32[2,3,8,128]{3,2,1,0:T(8,128)S(1)}, s32[2,3,8,128]{3,2,1,0:T(8,128)S(1)}, u32[]{:S(2)}, u32[]{:S(2)}) %collective-permute-start) | collective-permute-done | bytes 24608 | tf_op jit(solution)/shard_map/ppermute | solution.py:21
  16.7 2.4 %collective-permute-start.3 = (s32[2,12,3,128]{3,2,1,0:T(4,128)S(1)}, s32[2,12,3,128]{3,2,1,0:T(4,128)S(1)}, u32[]{:S(2)}, u32[]{:S(2)}) collective-permute-start(s32[2,12,3,128]{3,2,1,0:T(4,128)S(1)} %get-tuple-element.137), channel_id=1, source_target_pairs={{1,0},{3,2},{5,4},{7,6},{9,8},{11,10},{13,12},{15,14},{17,16},{19,... | collective-permute-start | bytes 110600 | tf_op jit(solution)/shard_map/ppermute | solution.py:23
  19.1 1.3 %collective-permute-start.2 = (s32[2,12,3,128]{3,2,1,0:T(4,128)S(1)}, s32[2,12,3,128]{3,2,1,0:T(4,128)S(1)}, u32[]{:S(2)}, u32[]{:S(2)}) collective-permute-start(s32[2,12,3,128]{3,2,1,0:T(4,128)S(1)} %get-tuple-element.136), channel_id=1, source_target_pairs={{0,1},{2,3},{4,5},{6,7},{8,9},{10,11},{12,13},{14,15},{16,17},{18,... | collective-permute-start | bytes 110600 | tf_op jit(solution)/shard_map/ppermute | solution.py:21
  20.5 4.5 %collective-permute-start.7 = (f32[3,12,3,128]{3,2,1,0:T(4,128)S(1)}, f32[3,12,3,128]{3,2,1,0:T(4,128)S(1)}, u32[]{:S(2)}, u32[]{:S(2)}) collective-permute-start(f32[3,12,3,128]{3,2,1,0:T(4,128)S(1)} %get-tuple-element.135), channel_id=1, source_target_pairs={{1,0},{3,2},{5,4},{7,6},{9,8},{11,10},{13,12},{15,14},{17,16},{19,... | collective-permute-start | bytes 165896 | tf_op jit(solution)/shard_map/ppermute | solution.py:23
  25.1 1.3 %collective-permute-start.6 = (f32[3,12,3,128]{3,2,1,0:T(4,128)S(1)}, f32[3,12,3,128]{3,2,1,0:T(4,128)S(1)}, u32[]{:S(2)}, u32[]{:S(2)}) collective-permute-start(f32[3,12,3,128]{3,2,1,0:T(4,128)S(1)} %get-tuple-element.134), channel_id=1, source_target_pairs={{0,1},{2,3},{4,5},{6,7},{8,9},{10,11},{12,13},{14,15},{16,17},{18,... | collective-permute-start | bytes 165896 | tf_op jit(solution)/shard_map/ppermute | solution.py:21
  27.0 4.3 %collective-permute-done.6 = f32[3,12,3,128]{3,2,1,0:T(4,128)S(1)} collective-permute-done((f32[3,12,3,128]{3,2,1,0:T(4,128)S(1)}, f32[3,12,3,128]{3,2,1,0:T(4,128)S(1)}, u32[]{:S(2)}, u32[]{:S(2)}) %collective-permute-start.6) | collective-permute-done | bytes 55328 | tf_op jit(solution)/shard_map/ppermute | solution.py:21
  37.3 1.2 %add_bitcast_fusion.3 = f32[1,12,14,128]{3,2,1,0:T(8,128)S(1)} fusion(f32[12,14,128]{2,1,0:T(8,128)S(1)} %get-tuple-element.127, f32[12,14,128]{2,1,0:T(8,128)S(1)} %get-tuple-element.126, f32[12,14,128]{2,1,0:T(8,128)S(1)} %get-tuple-element.125, f32[12,14,128]{2,1,0:T(8,128)S(1)} %get-tuple-element.131, f32[12,14,128]{2,1,0:T(8,128)S(1)} %get-tuple-element.124, ...), kind=kLoop, calls=%fused_computation.1661 | loop fusion | flops 3634176 | bytes 5332992 | tf_op jit(solution)/shard_map/stack | solution.py:96
  38.5 1.2 %add_bitcast_fusion.5 = (f32[1,12,14,128]{3,2,1,0:T(8,128)S(1)}, f32[12,14,128]{2,1,0:T(8,128)S(1)}) fusion(f32[12,14,128]{2,1,0:T(8,128)S(1)} %get-tuple-element.131, f32[12,14,128]{2,1,0:T(8,128)S(1)} %get-tuple-element.124, f32[12,14,128]{2,1,0:T(8,128)S(1)} %get-tuple-element.123, f32[12,14,128]{2,1,0:T(8,128)S(1)} %get-tuple-element.122, ...), kind=kLoop, calls=%fused_computation.1663 | loop fusion | flops 3333120 | bytes 5419008 | tf_op jit(solution)/shard_map/stack | solution.py:96
  39.8 1.1 %add_bitcast_fusion.4 = f32[1,12,14,128]{3,2,1,0:T(8,128)S(1)} fusion(f32[12,14,128]{2,1,0:T(8,128)S(1)} %get-tuple-element.9, f32[12,14,128]{2,1,0:T(8,128)S(1)} %get-tuple-element.131, f32[12,14,128]{2,1,0:T(8,128)S(1)} %get-tuple-element.124, f32[12,14,128]{2,1,0:T(8,128)S(1)} %get-tuple-element.123, f32[12,14,128]{2,1,0:T(8,128)S(1)} %get-tuple-element.122, ...), kind=kLoop, calls=%fused_computation.1662 | loop fusion | flops 3419136 | bytes 5160960 | tf_op jit(solution)/shard_map/stack | solution.py:96
  41.0 1.9 %collective-permute-start.9 = (f32[3,3,8,128]{3,2,1,0:T(8,128)S(1)}, f32[3,3,8,128]{3,2,1,0:T(8,128)S(1)}, u32[]{:S(2)}, u32[]{:S(2)}) collective-permute-start(f32[3,3,8,128]{3,2,1,0:T(8,128)S(1)} %get-tuple-element.139), channel_id=1, source_target_pairs={{2,0},{4,2},{6,4},{8,6},{10,8},{12,10},{14,12},{16,14},{18,16},{20... | collective-permute-start | bytes 110600 | tf_op jit(solution)/shard_map/ppermute | solution.py:23
  42.9 2.4 %collective-permute-start.8 = (f32[3,3,8,128]{3,2,1,0:T(8,128)S(1)}, f32[3,3,8,128]{3,2,1,0:T(8,128)S(1)}, u32[]{:S(2)}, u32[]{:S(2)}) collective-permute-start(f32[3,3,8,128]{3,2,1,0:T(8,128)S(1)} %get-tuple-element.138), channel_id=1, source_target_pairs={{0,2},{2,4},{4,6},{6,8},{8,10},{10,12},{12,14},{14,16},{16,18},{18... | collective-permute-start | bytes 110600 | tf_op jit(solution)/shard_map/ppermute | solution.py:21
  45.4 3.8 %collective-permute-done.8 = f32[3,3,8,128]{3,2,1,0:T(8,128)S(1)} collective-permute-done((f32[3,3,8,128]{3,2,1,0:T(8,128)S(1)}, f32[3,3,8,128]{3,2,1,0:T(8,128)S(1)}, u32[]{:S(2)}, u32[]{:S(2)}) %collective-permute-start.8) | collective-permute-done | bytes 36896 | tf_op jit(solution)/shard_map/ppermute | solution.py:21
  49.2 1.6 %collective-permute-start.11 = (f32[3,12,3,128]{3,2,1,0:T(4,128)S(1)}, f32[3,12,3,128]{3,2,1,0:T(4,128)S(1)}, u32[]{:S(2)}, u32[]{:S(2)}) collective-permute-start(f32[3,12,3,128]{3,2,1,0:T(4,128)S(1)} %get-tuple-element.133), channel_id=1, source_target_pairs={{1,0},{3,2},{5,4},{7,6},{9,8},{11,10},{13,12},{15,14},{17,16},{19,... | collective-permute-start | bytes 165896 | tf_op jit(solution)/shard_map/ppermute | solution.py:23
  50.7 1.5 %collective-permute-start.10 = (f32[3,12,3,128]{3,2,1,0:T(4,128)S(1)}, f32[3,12,3,128]{3,2,1,0:T(4,128)S(1)}, u32[]{:S(2)}, u32[]{:S(2)}) collective-permute-start(f32[3,12,3,128]{3,2,1,0:T(4,128)S(1)} %get-tuple-element.132), channel_id=1, source_target_pairs={{0,1},{2,3},{4,5},{6,7},{8,9},{10,11},{12,13},{14,15},{16,17},{18,... | collective-permute-start | bytes 165896 | tf_op jit(solution)/shard_map/ppermute | solution.py:21
  52.7 4.3 %collective-permute-done.10 = f32[3,12,3,128]{3,2,1,0:T(4,128)S(1)} collective-permute-done((f32[3,12,3,128]{3,2,1,0:T(4,128)S(1)}, f32[3,12,3,128]{3,2,1,0:T(4,128)S(1)}, u32[]{:S(2)}, u32[]{:S(2)}) %collective-permute-start.10) | collective-permute-done | bytes 55328 | tf_op jit(solution)/shard_map/ppermute | solution.py:21
  62.9 1.3 %add_bitcast_fusion = f32[1,12,14,128]{3,2,1,0:T(8,128)S(1)} fusion(f32[12,14,128]{2,1,0:T(8,128)S(1)} %get-tuple-element.68, f32[12,14,128]{2,1,0:T(8,128)S(1)} %get-tuple-element.67, f32[12,14,128]{2,1,0:T(8,128)S(1)} %get-tuple-element.66, f32[12,14,128]{2,1,0:T(8,128)S(1)} %get-tuple-element.129, f32[12,14,128]{2,1,0:T(8,128)S(1)} %get-tuple-element.65, ...), kind=kLoop, calls=%fused_computation.1658 | loop fusion | flops 3634176 | bytes 5332992 | tf_op jit(solution)/shard_map/stack | solution.py:96
  64.2 1.3 %add_bitcast_fusion.2 = (f32[1,12,14,128]{3,2,1,0:T(8,128)S(1)}, f32[12,14,128]{2,1,0:T(8,128)S(1)}) fusion(f32[12,14,128]{2,1,0:T(8,128)S(1)} %get-tuple-element.129, f32[12,14,128]{2,1,0:T(8,128)S(1)} %get-tuple-element.65, f32[12,14,128]{2,1,0:T(8,128)S(1)} %get-tuple-element.64, f32[12,14,128]{2,1,0:T(8,128)S(1)} %get-tuple-element.63, ...), kind=kLoop, calls=%fused_computation.1660 | loop fusion | flops 3333120 | bytes 5419008 | tf_op jit(solution)/shard_map/stack | solution.py:96
  65.5 1.2 %add_bitcast_fusion.1 = f32[1,12,14,128]{3,2,1,0:T(8,128)S(1)} fusion(f32[12,14,128]{2,1,0:T(8,128)S(1)} %get-tuple-element.5, f32[12,14,128]{2,1,0:T(8,128)S(1)} %get-tuple-element.129, f32[12,14,128]{2,1,0:T(8,128)S(1)} %get-tuple-element.65, f32[12,14,128]{2,1,0:T(8,128)S(1)} %get-tuple-element.64, f32[12,14,128]{2,1,0:T(8,128)S(1)} %get-tuple-element.63, ...), kind=kLoop, calls=%fused_computation.1659 | loop fusion | flops 3419136 | bytes 5160960 | tf_op jit(solution)/shard_map/stack | solution.py:96
  (92 shorter events, 14.6 us)
Async XLA Ops:
  0.6 16.0 %copy-start.1 = (s32[6,8,128]{2,1,0:T(8,128)S(1)}, s32[6,8,128]{2,1,0:T(8,128)}, u32[]{:S(2)}) copy-start(s32[6,8,128]{2,1,0:T(8,128)} %param.7) | copy-start | bytes 73732
  0.6 16.0 %copy-start.2 = (s32[6,8,128]{2,1,0:T(8,128)S(1)}, s32[6,8,128]{2,1,0:T(8,128)}, u32[]{:S(2)}) copy-start(s32[6,8,128]{2,1,0:T(8,128)} %param.8) | copy-start | bytes 73732
  1.5 19.0 %collective-permute-start.4 = (f32[3,3,8,128]{3,2,1,0:T(8,128)S(1)}, f32[3,3,8,128]{3,2,1,0:T(8,128)S(1)}, u32[]{:S(2)}, u32[]{:S(2)}) collective-permute-start(f32[3,3,8,128]{3,2,1,0:T(8,128)S(1)} %get-tuple-element.141), channel_id=1, source_target_pairs={{0,2},{2,4},{4,6},{6,8},{8,10},{10,12},{12,14},{14,16},{16,18},{18... | collective-permute-start | bytes 110600 | tf_op jit(solution)/shard_map/ppermute | solution.py:21
  3.4 17.1 %collective-permute-start.5 = (f32[3,3,8,128]{3,2,1,0:T(8,128)S(1)}, f32[3,3,8,128]{3,2,1,0:T(8,128)S(1)}, u32[]{:S(2)}, u32[]{:S(2)}) collective-permute-start(f32[3,3,8,128]{3,2,1,0:T(8,128)S(1)} %get-tuple-element.140), channel_id=1, source_target_pairs={{2,0},{4,2},{6,4},{8,6},{10,8},{12,10},{14,12},{16,14},{18,16},{20... | collective-permute-start | bytes 110600 | tf_op jit(solution)/shard_map/ppermute | solution.py:23
  8.7 5.4 %collective-permute-start.1 = (s32[2,3,8,128]{3,2,1,0:T(8,128)S(1)}, s32[2,3,8,128]{3,2,1,0:T(8,128)S(1)}, u32[]{:S(2)}, u32[]{:S(2)}) collective-permute-start(s32[2,3,8,128]{3,2,1,0:T(8,128)S(1)} %get-tuple-element.143), channel_id=1, source_target_pairs={{2,0},{4,2},{6,4},{8,6},{10,8},{12,10},{14,12},{16,14},{18,16},{20... | collective-permute-start | bytes 73736 | tf_op jit(solution)/shard_map/ppermute | solution.py:23
  10.6 6.0 %collective-permute-start = (s32[2,3,8,128]{3,2,1,0:T(8,128)S(1)}, s32[2,3,8,128]{3,2,1,0:T(8,128)S(1)}, u32[]{:S(2)}, u32[]{:S(2)}) collective-permute-start(s32[2,3,8,128]{3,2,1,0:T(8,128)S(1)} %get-tuple-element.142), channel_id=1, source_target_pairs={{0,2},{2,4},{4,6},{6,8},{8,10},{10,12},{12,14},{14,16},{16,18},{18... | collective-permute-start | bytes 73736 | tf_op jit(solution)/shard_map/ppermute | solution.py:21
  14.0 6.4 %copy-start = (f32[3,6,8,128]{3,2,1,0:T(8,128)S(1)}, f32[3,6,8,128]{3,2,1,0:T(8,128)}, u32[]{:S(2)}) copy-start(f32[3,6,8,128]{3,2,1,0:T(8,128)} %param.5) | copy-start | bytes 221188
  16.7 9.7 %collective-permute-start.3 = (s32[2,12,3,128]{3,2,1,0:T(4,128)S(1)}, s32[2,12,3,128]{3,2,1,0:T(4,128)S(1)}, u32[]{:S(2)}, u32[]{:S(2)}) collective-permute-start(s32[2,12,3,128]{3,2,1,0:T(4,128)S(1)} %get-tuple-element.137), channel_id=1, source_target_pairs={{1,0},{3,2},{5,4},{7,6},{9,8},{11,10},{13,12},{15,14},{17,16},{19,... | collective-permute-start | bytes 110600 | tf_op jit(solution)/shard_map/ppermute | solution.py:23
  19.1 7.3 %collective-permute-start.2 = (s32[2,12,3,128]{3,2,1,0:T(4,128)S(1)}, s32[2,12,3,128]{3,2,1,0:T(4,128)S(1)}, u32[]{:S(2)}, u32[]{:S(2)}) collective-permute-start(s32[2,12,3,128]{3,2,1,0:T(4,128)S(1)} %get-tuple-element.136), channel_id=1, source_target_pairs={{0,1},{2,3},{4,5},{6,7},{8,9},{10,11},{12,13},{14,15},{16,17},{18,... | collective-permute-start | bytes 110600 | tf_op jit(solution)/shard_map/ppermute | solution.py:21
  20.5 6.5 %collective-permute-start.7 = (f32[3,12,3,128]{3,2,1,0:T(4,128)S(1)}, f32[3,12,3,128]{3,2,1,0:T(4,128)S(1)}, u32[]{:S(2)}, u32[]{:S(2)}) collective-permute-start(f32[3,12,3,128]{3,2,1,0:T(4,128)S(1)} %get-tuple-element.135), channel_id=1, source_target_pairs={{1,0},{3,2},{5,4},{7,6},{9,8},{11,10},{13,12},{15,14},{17,16},{19,... | collective-permute-start | bytes 165896 | tf_op jit(solution)/shard_map/ppermute | solution.py:23
  25.1 6.2 %collective-permute-start.6 = (f32[3,12,3,128]{3,2,1,0:T(4,128)S(1)}, f32[3,12,3,128]{3,2,1,0:T(4,128)S(1)}, u32[]{:S(2)}, u32[]{:S(2)}) collective-permute-start(f32[3,12,3,128]{3,2,1,0:T(4,128)S(1)} %get-tuple-element.134), channel_id=1, source_target_pairs={{0,1},{2,3},{4,5},{6,7},{8,9},{10,11},{12,13},{14,15},{16,17},{18,... | collective-permute-start | bytes 165896 | tf_op jit(solution)/shard_map/ppermute | solution.py:21
  39.7 1.2 %copy-start.3 = (f32[3,6,8,128]{3,2,1,0:T(8,128)S(1)}, f32[3,6,8,128]{3,2,1,0:T(8,128)}, u32[]{:S(2)}) copy-start(f32[3,6,8,128]{3,2,1,0:T(8,128)} %param.6) | copy-start | bytes 221188
  41.0 4.3 %collective-permute-start.9 = (f32[3,3,8,128]{3,2,1,0:T(8,128)S(1)}, f32[3,3,8,128]{3,2,1,0:T(8,128)S(1)}, u32[]{:S(2)}, u32[]{:S(2)}) collective-permute-start(f32[3,3,8,128]{3,2,1,0:T(8,128)S(1)} %get-tuple-element.139), channel_id=1, source_target_pairs={{2,0},{4,2},{6,4},{8,6},{10,8},{12,10},{14,12},{16,14},{18,16},{20... | collective-permute-start | bytes 110600 | tf_op jit(solution)/shard_map/ppermute | solution.py:23
  42.9 6.2 %collective-permute-start.8 = (f32[3,3,8,128]{3,2,1,0:T(8,128)S(1)}, f32[3,3,8,128]{3,2,1,0:T(8,128)S(1)}, u32[]{:S(2)}, u32[]{:S(2)}) collective-permute-start(f32[3,3,8,128]{3,2,1,0:T(8,128)S(1)} %get-tuple-element.138), channel_id=1, source_target_pairs={{0,2},{2,4},{4,6},{6,8},{8,10},{10,12},{12,14},{14,16},{16,18},{18... | collective-permute-start | bytes 110600 | tf_op jit(solution)/shard_map/ppermute | solution.py:21
  49.2 3.5 %collective-permute-start.11 = (f32[3,12,3,128]{3,2,1,0:T(4,128)S(1)}, f32[3,12,3,128]{3,2,1,0:T(4,128)S(1)}, u32[]{:S(2)}, u32[]{:S(2)}) collective-permute-start(f32[3,12,3,128]{3,2,1,0:T(4,128)S(1)} %get-tuple-element.133), channel_id=1, source_target_pairs={{1,0},{3,2},{5,4},{7,6},{9,8},{11,10},{13,12},{15,14},{17,16},{19,... | collective-permute-start | bytes 165896 | tf_op jit(solution)/shard_map/ppermute | solution.py:23
  50.7 6.2 %collective-permute-start.10 = (f32[3,12,3,128]{3,2,1,0:T(4,128)S(1)}, f32[3,12,3,128]{3,2,1,0:T(4,128)S(1)}, u32[]{:S(2)}, u32[]{:S(2)}) collective-permute-start(f32[3,12,3,128]{3,2,1,0:T(4,128)S(1)} %get-tuple-element.132), channel_id=1, source_target_pairs={{0,1},{2,3},{4,5},{6,7},{8,9},{10,11},{12,13},{14,15},{16,17},{18,... | collective-permute-start | bytes 165896 | tf_op jit(solution)/shard_map/ppermute | solution.py:21
where the time goes:
time: 67.9 us; the launch traced here: 67.4 us
  starting transfers between devices  27.7 us (41%)
  other arithmetic  21.5 us (32%)
  waiting for transfers between devices  15.9 us (23%)
  between operations  1.35 us (2%)
  local copies, waits for them, and re-layouts  0.92 us (1%)
    ppermute x6, starting transfers between devices, with_halo(): lax.ppermute(head, axis, [((i + 1) % count, i) for i in range(ends)])  16.9 us
    ppermute x6, waiting for transfers between devices, with_halo(): lax.ppermute(tail, axis, [(i, (i + 1) % count) for i in range(ends)])  14.8 us
    mul x48, other arithmetic, bond_forces(): bond_term = modulus / length * intact * reach_mask * stretch  11.4 us
    ppermute x6, starting transfers between devices, with_halo(): lax.ppermute(tail, axis, [(i, (i + 1) % count) for i in range(ends)])  10.8 us
    another operation x6, other arithmetic, bond_forces(): return jnp.stack([force_x, force_y, force_z])  7.31 us
  transfers between devices with their start and end apart: 12, of which 6 were waited for; matrix products, arithmetic and copies ran while one was open for 3% of the time, Pallas kernels for 0%

commit v1 on v0

v1 whole, which is shorter than its diff:
```python
import functools

import jax
import jax.numpy as jnp
from jax import lax
from jax.experimental import pallas as pl
from jax.experimental.pallas import tpu as pltpu
from jax.sharding import PartitionSpec as P

STEPS = 2
REACH = 3
MODULUS = 0.1
TIME_STEP = 0.5
WORD = 31
MESH = pl.DeviceIdType.MESH
ROW = 8


def bond_offsets():
    found = []
    for a in range(-REACH, REACH + 1):
        for b in range(-REACH, REACH + 1):
            for c in range(-REACH, REACH + 1):
                square = a * a + b * b + c * c
                if 0 < square <= REACH * REACH and (a, b, c) > (0, 0, 0):
                    found.append((a, b, c))
    return found


BONDS = {offset: number for number, offset in enumerate(bond_offsets())}
DIRECTED = {}
for _offset, _number in BONDS.items():
    DIRECTED[_offset] = (_number, True)
    DIRECTED[tuple(-v for v in _offset)] = (_number, False)
COLUMNS = sorted({(b, c) for _, b, c in DIRECTED}, key=lambda bc: (abs(bc[0]), bc))
ALONG = {bc: sorted(a for a, b, c in DIRECTED if (b, c) == bc) for bc in COLUMNS}
SLOT = {offset: place for place, offset in enumerate(sorted(DIRECTED))}


def word_bits(test):
    words = [0, 0]
    for offset, number in BONDS.items():
        if test(offset):
            words[number // WORD] |= 1 << (number % WORD)
    return words


def times(factor, value):
    if factor == 1:
        return value
    if factor == -1:
        return -value
    return float(factor) * value


def plus_times(total, factor, value):
    if factor == 0:
        return total
    if total is None:
        return times(factor, value)
    if factor == 1:
        return total + value
    if factor == -1:
        return total - value
    return total + float(factor) * value


def add_planes(total, start, value):
    count = total.shape[0]
    stop = start + value.shape[0]
    parts = []
    if start > 0:
        parts.append(total[:start])
    parts.append(total[start:stop] + value)
    if stop < count:
        parts.append(total[stop:])
    return parts[0] if len(parts) == 1 else jnp.concatenate(parts, axis=0)


def kernel(
    n_bar,
    n_lat,
    u_ref,
    v_ref,
    low_ref,
    high_ref,
    bc_ref,
    uo_ref,
    vo_ref,
    u_mid,
    field,
    flags,
    weight,
    pack_lat,
    pack_corner,
    pack_flag_lat,
    pack_flag_corner,
    got_bar,
    got_lat,
    got_corner,
    got_high,
    got_low,
    got_flag_lat,
    got_flag_corner,
    send_sem,
    recv_sem,
):
    size_x, size_y, size_z = u_ref.shape[1:]
    me_bar = lax.axis_index("bar")
    me_lat = lax.axis_index("lat")

    def there(d_bar, d_lat):
        ok = None
        for step, me, count in ((d_bar, me_bar, n_bar), (d_lat, me_lat, n_lat)):
            if step:
                good = me > 0 if step < 0 else me < count - 1
                ok = good if ok is None else jnp.logical_and(ok, good)
        return ok

    around = [(i, j) for i in (-1, 0, 1) for j in (-1, 0, 1) if (i, j) != (0, 0)]
    barrier = pltpu.get_barrier_semaphore()
    for i, j in around:

        @pl.when(there(i, j))
        def _():
            pl.semaphore_signal(barrier, inc=1, device_id=(me_bar + i, me_lat + j), device_id_type=MESH)

    def rows_of(side, width):
        return slice(0, width) if side == 0 else slice(size_y - width, size_y)

    def pack_moving(step, source):
        for side in range(2):
            for comp in range(3):
                for p in range(size_x):
                    at = (comp * size_x + p) * 3
                    pack_lat[step, side, at : at + 3, :] = source[comp, p, rows_of(side, 3), :]
                for end in range(2):
                    for q in range(2):
                        p = q if end == 0 else size_x - 2 + q
                        at = (comp * 2 + q) * 2
                        pack_corner[step, end, side, at : at + 2, :] = source[comp, p, rows_of(side, 2), :]

    words = (low_ref, high_ref)
    for side in range(2):
        for w in range(2):
            for p in range(size_x):
                at = (w * size_x + p) * 3
                pack_flag_lat[side, at : at + 3, :] = words[w][p, rows_of(side, 3), :]
        for at, (w, p) in enumerate(((0, size_x - 1), (1, size_x - 2), (1, size_x - 1))):
            pack_flag_corner[side, 2 * at : 2 * at + 2, :] = words[w][p, rows_of(side, 2), :]
    pack_moving(0, u_ref)

    for end in range(2):

        @pl.when(jnp.logical_not(there(2 * end - 1, 0)))
        def _():
            for step in range(STEPS):
                got_bar[step, end] = jnp.zeros(got_bar.shape[2:], jnp.float32)

        @pl.when(jnp.logical_not(there(0, 2 * end - 1)))
        def _():
            for step in range(STEPS):
                got_lat[step, end] = jnp.zeros(got_lat.shape[2:], jnp.float32)
            got_flag_lat[end] = jnp.full(got_flag_lat.shape[1:], -1, jnp.int32)

        for side in range(2):

            @pl.when(jnp.logical_not(there(2 * end - 1, 2 * side - 1)))
            def _():
                for step in range(STEPS):
                    got_corner[step, end, side] = jnp.zeros(got_corner.shape[3:], jnp.float32)
                if end == 0:
                    got_flag_corner[side] = jnp.full(got_flag_corner.shape[1:], -1, jnp.int32)

    @pl.when(jnp.logical_not(there(-1, 0)))
    def _():
        got_high[...] = jnp.full(got_high.shape, -1, jnp.int32)
        got_low[...] = jnp.full(got_low.shape, -1, jnp.int32)

    copies = []

    def post(group, source, target, i, j):
        place = len(copies)
        copy = pltpu.make_async_remote_copy(
            src_ref=source,
            dst_ref=target,
            send_sem=send_sem.at[place],
            recv_sem=recv_sem.at[place],
            device_id=(me_bar + i, me_lat + j),
            device_id_type=MESH,
        )

        @pl.when(there(i, j))
        def _():
            copy.start()

        copies.append((group, copy, (i, j)))

    def send_moving(step, source):
        for side in range(2):
            post((step, "lat"), pack_lat.at[step, side], got_lat.at[step, 1 - side], 0, 2 * side - 1)
        for end in range(2):
            first = 0 if end == 0 else size_x - 3
            post((step, "bar"), source.at[:, first : first + 3], got_bar.at[step, 1 - end], 2 * end - 1, 0)
            for side in range(2):
                post(
                    (step, "bar"),
                    pack_corner.at[step, end, side],
                    got_corner.at[step, 1 - end, 1 - side],
                    2 * end - 1,
                    2 * side - 1,
                )

    def wait(group):
        for name, copy, (i, j) in copies:
            if name == group:

                @pl.when(there(-i, -j))
                def _():
                    copy.wait_recv()

    span_bar = (me_bar > 0).astype(jnp.int32) + (me_bar < n_bar - 1).astype(jnp.int32)
    span_lat = (me_lat > 0).astype(jnp.int32) + (me_lat < n_lat - 1).astype(jnp.int32)
    pl.semaphore_wait(barrier, (span_bar + 1) * (span_lat + 1) - 1)

    for side in range(2):
        post((0, "lat"), pack_flag_lat.at[side], got_flag_lat.at[1 - side], 0, 2 * side - 1)
    post((0, "bar"), high_ref.at[size_x - 3 :], got_high, 1, 0)
    post((0, "bar"), low_ref.at[size_x - 1 :], got_low, 1, 0)
    for side in range(2):
        post((0, "bar"), pack_flag_corner.at[side], got_flag_corner.at[1 - side], 1, 2 * side - 1)
    send_moving(0, u_ref)

    lane = lax.broadcasted_iota(jnp.int32, (size_y, size_z), 1)
    row = lax.broadcasted_iota(jnp.int32, (size_y, size_z), 0) + me_lat * size_y
    zero = jnp.zeros((size_y, size_z), jnp.int32)
    leave_z, leave_y = [zero, zero], [zero, zero]
    for d in (-3, -2, -1, 1, 2, 3):
        bits = word_bits(lambda o: o[2] == d)
        gone = (lane + d < 0) | (lane + d >= size_z)
        leave_z = [m | jnp.where(gone, x, 0) for m, x in zip(leave_z, bits)]
        bits = word_bits(lambda o: o[1] == d)
        gone = (row + d < 0) | (row + d >= size_y * n_lat)
        leave_y = [m | jnp.where(gone, x, 0) for m, x in zip(leave_y, bits)]
    last = me_bar == n_bar - 1

    def rolled(value, c):
        return value if c == 0 else pltpu.roll(value, (-c) % size_z, axis=value.ndim - 1)

    def fill_rows(buffer, lead, value, c):
        buffer[(c + 3,) + lead + (slice(ROW, ROW + size_y),)] = rolled(value, c)

    def fill_halo(buffer, lead, value, c):
        moved = rolled(value, c)
        buffer[(c + 3,) + lead + (slice(0, ROW),)] = moved
        buffer[(c + 3,) + lead + (slice(ROW + size_y, 2 * ROW + size_y),)] = moved

    def halo_of(buffer, lead):
        return buffer[(3,) + lead + (slice(0, ROW),)]

    for w in range(2):
        for p in range(size_x):
            leave_x = word_bits(lambda o: o[0] + p >= size_x)[w]
            word = words[w][p] | leave_z[w] | leave_y[w] | jnp.where(last, leave_x, 0)
            for c in range(-3, 4):
                fill_rows(flags, (w, 3 + p), word, c)

    planes = slice(3, 3 + size_x)

    def fill_own(source):
        for comp in range(3):
            value = source[comp]
            for c in range(-3, 4):
                fill_rows(field, (comp, planes), value, c)

    def flag_at(c, w, lead, rows):
        return flags[c + 3, w, lead, rows, :]

    def weights(step, offset, start, stop):
        place = SLOT[offset]
        if step > 0:
            return weight[place, start:stop]
        number, forward = DIRECTED[offset]
        a, b, c = offset
        w, bit = number // WORD, 1 << (number % WORD)
        if forward:
            word = flags[3, w, 3 + start : 3 + stop, ROW : ROW + size_y, :]
        else:
            word = flags[c + 3, w, 3 + start + a : 3 + stop + a, ROW + b : ROW + b + size_y, :]
        value = MODULUS / float(a * a + b * b + c * c) ** 1.5
        found = jnp.where((word & bit) == 0, jnp.float32(value), jnp.float32(0.0))
        weight[place, start:stop] = found
        return found

    def near(comp, b, c, start, stop):
        return field[c + 3, comp, 3 + start : 3 + stop, ROW + b : ROW + b + size_y, :]

    def inner(step, columns, force):
        for b, c in columns:
            mine, other = None, None
            for comp, factor in ((1, b), (2, c)):
                if factor:
                    mine = plus_times(mine, factor, near(comp, 0, 0, 0, size_x))
                    other = plus_times(other, factor, near(comp, b, c, 0, size_x))
            mine_x = near(0, 0, 0, 0, size_x)
            other_x = near(0, b, c, 0, size_x)
            total, total_x = None, None
            for a in sorted(ALONG[b, c], key=abs):
                start, stop = max(0, -a), min(size_x, size_x - a)
                if mine is None:
                    stretch = times(a, other_x[start + a : stop + a] - mine_x[start:stop])
                else:
                    stretch = plus_times(other[start + a : stop + a], a, other_x[start + a : stop + a])
                    stretch = stretch - plus_times(mine[start:stop], a, mine_x[start:stop])
                term = weights(step, (a, b, c), start, stop) * stretch
                if mine is not None:
                    total = term if total is None else add_planes(total, start, term)
                if a:
                    if total_x is None:
                        total_x = jnp.zeros((size_x, size_y, size_z), jnp.float32)
                    total_x = add_planes(total_x, start, times(a, term))
            if total_x is not None:
                force[0] = force[0] + total_x
            for comp, factor in ((1, b), (2, c)):
                force[comp] = plus_times(force[comp], factor, total) if factor else force[comp]

    def outer(step, force):
        for b, c in COLUMNS:
            for end in range(2):
                for a in ALONG[b, c]:
                    if a == 0 or (a > 0) != (end == 1):
                        continue
                    start, stop = (0, -a) if a < 0 else (size_x - a, size_x)
                    stretch = None
                    for comp, factor in ((0, a), (1, b), (2, c)):
                        if factor:
                            change = near(comp, b, c, start + a, stop + a) - near(comp, 0, 0, start, stop)
                            stretch = plus_times(stretch, factor, change)
                    term = weights(step, (a, b, c), start, stop) * stretch
                    for comp, factor in ((0, a), (1, b), (2, c)):
                        if factor:
                            force[comp] = add_planes(force[comp], start, times(factor, term))

    code = bc_ref[me_bar].astype(jnp.float32)
    retain = 1.0 - 0.2 * code

    flat = [bc for bc in COLUMNS if bc[0] == 0]
    tilted = [bc for bc in COLUMNS if bc[0] != 0]
    for step in range(STEPS):
        source = u_ref if step == 0 else u_mid
        old_v = v_ref if step == 0 else vo_ref
        fill_own(source)
        force = [jnp.zeros((size_x, size_y, size_z), jnp.float32)] * 3
        inner(step, flat, force)

        wait((step, "lat"))
        if step == 0:
            for w in range(2):
                for p in range(size_x):
                    at = (w * size_x + p) * 3
                    flags[3, w, 3 + p, ROW - 3 : ROW, :] = got_flag_lat[0, at : at + 3, :]
                    flags[3, w, 3 + p, 0:3, :] = got_flag_lat[1, at : at + 3, :]
                    value = halo_of(flags, (w, 3 + p)) | leave_z[w]
                    for c in range(-2, 3):
                        fill_halo(flags, (w, 3 + p), value, c)
        for comp in range(3):
            for p in range(size_x):
                at = (comp * size_x + p) * 3
                field[3, comp, 3 + p, ROW - 3 : ROW, :] = got_lat[step, 0, at : at + 3, :]
                field[3, comp, 3 + p, 0:3, :] = got_lat[step, 1, at : at + 3, :]
            value = halo_of(field, (comp, planes))
            for c in range(-2, 3):
                fill_halo(field, (comp, planes), value, c)
        inner(step, tilted, force)

        wait((step, "bar"))
        if step == 0:
            for at, (w, q) in enumerate(((0, 2), (1, 1), (1, 2))):
                flags[3, w, q, ROW - 2 : ROW, :] = got_flag_corner[0, 2 * at : 2 * at + 2, :]
                flags[3, w, q, 0:2, :] = got_flag_corner[1, 2 * at : 2 * at + 2, :]
                own = got_low[0] if w == 0 else got_high[q]
                own = own | leave_z[w]
                value = halo_of(flags, (w, q)) | leave_z[w]
                for c in range(-2, 3):
                    fill_rows(flags, (w, q), own, c)
                    fill_halo(flags, (w, q), value, c)
            fill_rows(flags, (1, 0), got_high[0], 0)
        for comp in range(3):
            for end in range(2):
                first = 1 if end == 0 else 3 + size_x
                for q in range(2):
                    at = (comp * 2 + q) * 2
                    field[3, comp, first + q, ROW - 2 : ROW, :] = got_corner[step, end, 0, at : at + 2, :]
                    field[3, comp, first + q, 0:2, :] = got_corner[step, end, 1, at : at + 2, :]
                lead = (comp, slice(first, first + 2))
                value = halo_of(field, lead)
                own = got_bar[step, end, comp, 1 - end : 3 - end]
                for c in range(-2, 3):
                    fill_halo(field, lead, value, c)
                    fill_rows(field, lead, own, c)
                far = 0 if end == 0 else 5 + size_x
                fill_rows(field, (comp, far), got_bar[step, end, comp, 2 * end], 0)
        outer(step, force)

        for comp in range(3):
            fast = retain * (old_v[comp] + TIME_STEP * force[comp])
            moved = source[comp] + TIME_STEP * fast
            vo_ref[comp] = fast
            if step == STEPS - 1:
                uo_ref[comp] = moved
            else:
                u_mid[comp] = moved
        if step < STEPS - 1:
            pack_moving(step + 1, u_mid)
            send_moving(step + 1, u_mid)

    for _, copy, (i, j) in copies:

        @pl.when(there(i, j))
        def _():
            copy.wait_send()


def local(n_bar, n_lat, displace, velocity, bond_low, bond_high, bc_type):
    _, size_x, size_y, size_z = displace.shape

    def up(rows):
        return -(-rows // 8) * 8

    rows_lat, rows_corner, rows_flag = up(9 * size_x), up(12), up(6 * size_x)
    copies = 6 + 8 * STEPS
    vmem = pl.BlockSpec(memory_space=pltpu.VMEM)
    return pl.pallas_call(
        functools.partial(kernel, n_bar, n_lat),
        out_shape=(
            jax.ShapeDtypeStruct(displace.shape, jnp.float32),
            jax.ShapeDtypeStruct(velocity.shape, jnp.float32),
        ),
        in_specs=[vmem] * 4 + [pl.BlockSpec(memory_space=pltpu.SMEM)],
        out_specs=(vmem, vmem),
        scratch_shapes=[
            pltpu.VMEM(displace.shape, jnp.float32),
            pltpu.VMEM((7, 3, size_x + 6, size_y + 16, size_z), jnp.float32),
            pltpu.VMEM((7, 2, size_x + 3, size_y + 16, size_z), jnp.int32),
            pltpu.VMEM((len(DIRECTED), size_x, size_y, size_z), jnp.float32),
            pltpu.VMEM((STEPS, 2, rows_lat, size_z), jnp.float32),
            pltpu.VMEM((STEPS, 2, 2, rows_corner, size_z), jnp.float32),
            pltpu.VMEM((2, rows_flag, size_z), jnp.int32),
            pltpu.VMEM((2, 8, size_z), jnp.int32),
            pltpu.VMEM((STEPS, 2, 3, 3, size_y, size_z), jnp.float32),
            pltpu.VMEM((STEPS, 2, rows_lat, size_z), jnp.float32),
            pltpu.VMEM((STEPS, 2, 2, rows_corner, size_z), jnp.float32),
            pltpu.VMEM((3, size_y, size_z), jnp.int32),
            pltpu.VMEM((1, size_y, size_z), jnp.int32),
            pltpu.VMEM((2, rows_flag, size_z), jnp.int32),
            pltpu.VMEM((2, 8, size_z), jnp.int32),
            pltpu.SemaphoreType.DMA((copies,)),
            pltpu.SemaphoreType.DMA((copies,)),
        ],
        compiler_params=pltpu.CompilerParams(collective_id=0, has_side_effects=True),
        name="leapfrog",
    )(displace, velocity, bond_low, bond_high, bc_type)


def solution(mesh):
    cells = P(None, "bar", "lat", None)
    return jax.shard_map(
        functools.partial(local, mesh.shape["bar"], mesh.shape["lat"]),
        mesh=mesh,
        in_specs=(cells, cells, P("bar", "lat", None), P("bar", "lat", None), P()),
        out_specs=(cells, cells),
        check_vma=False,
    )
```

time: 67.9 us -> 16.3 us (0.24)
  the two profiles are of different devices: /device:TPU:12 before, /device:TPU:0 now
where the time goes in v1:
time: 16.3 us; the launch traced here: 16.1 us
  Pallas kernels  13.3 us (82%)
  local copies, waits for them, and re-layouts  2.19 us (13%)
  between operations  0.65 us (4%)
    pallas_call x1, Pallas kernels, local(): pl.pallas_call(functools.partial(kernel, n_bar, n_lat), out_shape=(jax.Sh...  13.3 us
    unnamed x4, local copies, waits for them, and re-layouts  2.19 us

profile of v1, /device:TPU:0, one launch (start us, length us, event | category | flops | bytes accessed | tf_op | source)
XLA Modules:
  0.0 16.1 jit_solution(9460779278931882600)
XLA Ops:
  0.6 13.3 %leapfrog.1 = (f32[3,6,8,128]{3,2,1,0:T(8,128)}, f32[3,6,8,128]{3,2,1,0:T(8,128)}) custom-call(f32[3,6,8,128]{3,2,1,0:T(8,128)} %u_ref.1, f32[3,6,8,128]{3,2,1,0:T(8,128)} %v_ref.1, s32[6,8,128]{2,1,0:T(8,128)} %low_ref.1, s32[6,8,128]{2,1,0:T(8,128)} %high_ref.1, s32[16]{0:T(128)} %bc_ref.1), custom_call_target="tpu_custom_call" | custom-call | tf_op jit(solution)/shard_map/leapfrog/pallas_call | solution.py:433
  13.9 0.0 copy-start
  13.9 1.6 %copy.9 = f32[3,6,8,128]{3,2,1,0:T(8,128)} copy(f32[3,6,8,128]{3,2,1,0:T(8,128)} %get-tuple-element.4) | data formatting | bytes 147456
  15.5 0.0 copy-done
  15.5 0.6 %copy.10 = f32[3,6,8,128]{3,2,1,0:T(8,128)} copy(f32[3,6,8,128]{3,2,1,0:T(8,128)S(1)} %copy-done) | data formatting | bytes 147456
Async XLA Ops:
  13.9 1.6 %copy-start = (f32[3,6,8,128]{3,2,1,0:T(8,128)S(1)}, f32[3,6,8,128]{3,2,1,0:T(8,128)}, u32[]{:S(2)}) copy-start(f32[3,6,8,128]{3,2,1,0:T(8,128)} %get-tuple-element.5) | copy-start | bytes 221188

commit v2 on v1

--- a/solution.py
+++ b/solution.py
@@ -80,13 +80,17 @@
 def kernel(
     n_bar,
     n_lat,
+    u_in,
+    v_in,
+    low_in,
+    high_in,
+    bc_ref,
+    u_mid_out,
+    vo_ref,
     u_ref,
     v_ref,
     low_ref,
     high_ref,
-    bc_ref,
-    uo_ref,
-    vo_ref,
     u_mid,
     field,
     flags,
@@ -104,6 +108,7 @@
     got_flag_corner,
     send_sem,
     recv_sem,
+    load_sem,
 ):
     size_x, size_y, size_z = u_ref.shape[1:]
     me_bar = lax.axis_index("bar")
@@ -124,6 +129,15 @@
         @pl.when(there(i, j))
         def _():
             pl.semaphore_signal(barrier, inc=1, device_id=(me_bar + i, me_lat + j), device_id_type=MESH)
+
+    loads = [
+        pltpu.make_async_copy(source, target, load_sem.at[place])
+        for place, (source, target) in enumerate(
+            ((u_in, u_ref), (low_in, low_ref), (high_in, high_ref), (v_in, v_ref))
+        )
+    ]
+    for load in loads:
+        load.start()
 
     def rows_of(side, width):
         return slice(0, width) if side == 0 else slice(size_y - width, size_y)
@@ -140,6 +154,36 @@
                         at = (comp * 2 + q) * 2
                         pack_corner[step, end, side, at : at + 2, :] = source[comp, p, rows_of(side, 2), :]
 
+    for end in range(2):
+
+        @pl.when(jnp.logical_not(there(2 * end - 1, 0)))
+        def _():
+            for step in range(STEPS):
+                got_bar[step, end] = jnp.zeros(got_bar.shape[2:], jnp.float32)
+
+        @pl.when(jnp.logical_not(there(0, 2 * end - 1)))
+        def _():
+            for step in range(STEPS):
+                got_lat[step, end] = jnp.zeros(got_lat.shape[2:], jnp.float32)
+            got_flag_lat[end] = jnp.full(got_flag_lat.shape[1:], -1, jnp.int32)
+
+        for side in range(2):
+
+            @pl.when(jnp.logical_not(there(2 * end - 1, 2 * side - 1)))
+            def _():
+                for step in range(STEPS):
+                    got_corner[step, end, side] = jnp.zeros(got_corner.shape[3:], jnp.float32)
+                if end == 0:
+                    got_flag_corner[side] = jnp.full(got_flag_corner.shape[1:], -1, jnp.int32)
+
+    @pl.when(jnp.logical_not(there(-1, 0)))
+    def _():
+        got_high[...] = jnp.full(got_high.shape, -1, jnp.int32)
+        got_low[...] = jnp.full(got_low.shape, -1, jnp.int32)
+
+    for load in loads[:3]:
+        load.wait()
+    pack_moving(0, u_ref)
     words = (low_ref, high_ref)
     for side in range(2):
         for w in range(2):
@@ -148,34 +192,6 @@
                 pack_flag_lat[side, at : at + 3, :] = words[w][p, rows_of(side, 3), :]
         for at, (w, p) in enumerate(((0, size_x - 1), (1, size_x - 2), (1, size_x - 1))):
             pack_flag_corner[side, 2 * at : 2 * at + 2, :] = words[w][p, rows_of(side, 2), :]
-    pack_moving(0, u_ref)
-
-    for end in range(2):
-
-        @pl.when(jnp.logical_not(there(2 * end - 1, 0)))
-        def _():
-            for step in range(STEPS):
-                got_bar[step, end] = jnp.zeros(got_bar.shape[2:], jnp.float32)
-
-        @pl.when(jnp.logical_not(there(0, 2 * end - 1)))
-        def _():
-            for step in range(STEPS):
-                got_lat[step, end] = jnp.zeros(got_lat.shape[2:], jnp.float32)
-            got_flag_lat[end] = jnp.full(got_flag_lat.shape[1:], -1, jnp.int32)
-
-        for side in range(2):
-
-            @pl.when(jnp.logical_not(there(2 * end - 1, 2 * side - 1)))
-            def _():
-                for step in range(STEPS):
-                    got_corner[step, end, side] = jnp.zeros(got_corner.shape[3:], jnp.float32)
-                if end == 0:
-                    got_flag_corner[side] = jnp.full(got_flag_corner.shape[1:], -1, jnp.int32)
-
-    @pl.when(jnp.logical_not(there(-1, 0)))
-    def _():
-        got_high[...] = jnp.full(got_high.shape, -1, jnp.int32)
-        got_low[...] = jnp.full(got_low.shape, -1, jnp.int32)
 
     copies = []
 
@@ -197,11 +213,7 @@
         copies.append((group, copy, (i, j)))
 
     def send_moving(step, source):
-        for side in range(2):
-            post((step, "lat"), pack_lat.at[step, side], got_lat.at[step, 1 - side], 0, 2 * side - 1)
         for end in range(2):
-            first = 0 if end == 0 else size_x - 3
-            post((step, "bar"), source.at[:, first : first + 3], got_bar.at[step, 1 - end], 2 * end - 1, 0)
             for side in range(2):
                 post(
                     (step, "bar"),
@@ -210,6 +222,19 @@
                     2 * end - 1,
                     2 * side - 1,
                 )
+        if step == 0:
+            for side in range(2):
+                post((0, "bar"), pack_flag_corner.at[side], got_flag_corner.at[1 - side], 1, 2 * side - 1)
+        for side in range(2):
+            post((step, "lat"), pack_lat.at[step, side], got_lat.at[step, 1 - side], 0, 2 * side - 1)
+        for end in range(2):
+            first = 0 if end == 0 else size_x - 3
+            post((step, "bar"), source.at[:, first : first + 3], got_bar.at[step, 1 - end], 2 * end - 1, 0)
+        if step == 0:
+            for side in range(2):
+                post((0, "lat"), pack_flag_lat.at[side], got_flag_lat.at[1 - side], 0, 2 * side - 1)
+            post((0, "bar"), high_ref.at[size_x - 3 :], got_high, 1, 0)
+            post((0, "bar"), low_ref.at[size_x - 1 :], got_low, 1, 0)
 
     def wait(group):
         for name, copy, (i, j) in copies:
@@ -223,12 +248,6 @@
     span_lat = (me_lat > 0).astype(jnp.int32) + (me_lat < n_lat - 1).astype(jnp.int32)
     pl.semaphore_wait(barrier, (span_bar + 1) * (span_lat + 1) - 1)
 
-    for side in range(2):
-        post((0, "lat"), pack_flag_lat.at[side], got_flag_lat.at[1 - side], 0, 2 * side - 1)
-    post((0, "bar"), high_ref.at[size_x - 3 :], got_high, 1, 0)
-    post((0, "bar"), low_ref.at[size_x - 1 :], got_low, 1, 0)
-    for side in range(2):
-        post((0, "bar"), pack_flag_corner.at[side], got_flag_corner.at[1 - side], 1, 2 * side - 1)
     send_moving(0, u_ref)
 
     lane = lax.broadcasted_iota(jnp.int32, (size_y, size_z), 1)
@@ -403,13 +422,14 @@
         outer(step, force)
 
         for comp in range(3):
+            if step == 0 and comp == 0:
+                loads[3].wait()
             fast = retain * (old_v[comp] + TIME_STEP * force[comp])
-            moved = source[comp] + TIME_STEP * fast
             vo_ref[comp] = fast
             if step == STEPS - 1:
-                uo_ref[comp] = moved
+                u_mid_out[comp] = source[comp]
             else:
-                u_mid[comp] = moved
+                u_mid[comp] = source[comp] + TIME_STEP * fast
         if step < STEPS - 1:
             pack_moving(step + 1, u_mid)
             send_moving(step + 1, u_mid)
@@ -421,6 +441,12 @@
             copy.wait_send()
 
 
+def advance(u_ref, v_ref, uo_ref, vo_ref):
+    fast = v_ref[...]
+    uo_ref[...] = u_ref[...] + TIME_STEP * fast
+    vo_ref[...] = fast
+
+
 def local(n_bar, n_lat, displace, velocity, bond_low, bond_high, bc_type):
     _, size_x, size_y, size_z = displace.shape
 
@@ -430,15 +456,20 @@
     rows_lat, rows_corner, rows_flag = up(9 * size_x), up(12), up(6 * size_x)
     copies = 6 + 8 * STEPS
     vmem = pl.BlockSpec(memory_space=pltpu.VMEM)
-    return pl.pallas_call(
+    out_shape = (
+        jax.ShapeDtypeStruct(displace.shape, jnp.float32),
+        jax.ShapeDtypeStruct(velocity.shape, jnp.float32),
+    )
+    moved, fast = pl.pallas_call(
         functools.partial(kernel, n_bar, n_lat),
-        out_shape=(
-            jax.ShapeDtypeStruct(displace.shape, jnp.float32),
-            jax.ShapeDtypeStruct(velocity.shape, jnp.float32),
-        ),
-        in_specs=[vmem] * 4 + [pl.BlockSpec(memory_space=pltpu.SMEM)],
+        out_shape=out_shape,
+        in_specs=[pl.BlockSpec(memory_space=pl.ANY)] * 4 + [pl.BlockSpec(memory_space=pltpu.SMEM)],
         out_specs=(vmem, vmem),
         scratch_shapes=[
+            pltpu.VMEM(displace.shape, jnp.float32),
+            pltpu.VMEM(velocity.shape, jnp.float32),
+            pltpu.VMEM(bond_low.shape, jnp.int32),
+            pltpu.VMEM(bond_high.shape, jnp.int32),
             pltpu.VMEM(displace.shape, jnp.float32),
             pltpu.VMEM((7, 3, size_x + 6, size_y + 16, size_z), jnp.float32),
             pltpu.VMEM((7, 2, size_x + 3, size_y + 16, size_z), jnp.int32),
@@ -456,10 +487,18 @@
             pltpu.VMEM((2, 8, size_z), jnp.int32),
             pltpu.SemaphoreType.DMA((copies,)),
             pltpu.SemaphoreType.DMA((copies,)),
+            pltpu.SemaphoreType.DMA((4,)),
         ],
         compiler_params=pltpu.CompilerParams(collective_id=0, has_side_effects=True),
         name="leapfrog",
     )(displace, velocity, bond_low, bond_high, bc_type)
+    return pl.pallas_call(
+        advance,
+        out_shape=out_shape,
+        in_specs=[vmem] * 2,
+        out_specs=(vmem, vmem),
+        name="advance",
+    )(moved, fast)
 
 
 def solution(mesh):

time: 16.3 us -> 15.8 us (0.969)
  local copies, waits for them, and re-layouts: 2.19 us -> 0 us
  Pallas kernels: 13.3 us -> 14.9 us
    unnamed x4 -> x0, local copies, waits for them, and re-layouts: 2.19 us -> none
    pallas_call x1 -> x2, Pallas kernels: 13.3 us -> 14.9 us  [the longest x1 13.3 us: local(): pl.pallas_call(functools.partial(kernel, n_bar, n_lat), out_shape=out_sha...]
where the time goes in v2:
time: 15.8 us; the launch traced here: 15.6 us
  Pallas kernels  14.9 us (94%)
  between operations  0.64 us (4%)
    pallas_call x1, Pallas kernels, local(): pl.pallas_call(functools.partial(kernel, n_bar, n_lat), out_shape=out_sha...  13.3 us
    pallas_call x1, Pallas kernels, local(): pl.pallas_call(advance, out_shape=out_shape, in_specs=[vmem] * 2, out_spe...  1.59 us

profile of v2, /device:TPU:0, one launch (start us, length us, event | category | flops | bytes accessed | tf_op | source)
XLA Modules:
  0.0 15.6 jit_solution(14738285234818525180)
XLA Ops:
  0.6 13.3 %leapfrog.1 = (f32[3,6,8,128]{3,2,1,0:T(8,128)}, f32[3,6,8,128]{3,2,1,0:T(8,128)}) custom-call(f32[3,6,8,128]{3,2,1,0:T(8,128)} %u_in.1, f32[3,6,8,128]{3,2,1,0:T(8,128)} %v_in.1, s32[6,8,128]{2,1,0:T(8,128)} %low_in.1, s32[6,8,128]{2,1,0:T(8,128)} %high_in.1, s32[16]{0:T(128)} %bc_ref.1), custom_call_target="tpu_custom_call" | custom-call | tf_op jit(solution)/shard_map/leapfrog/pallas_call | solution.py:463
  14.0 1.6 %advance.1 = (f32[3,6,8,128]{3,2,1,0:T(8,128)}, f32[3,6,8,128]{3,2,1,0:T(8,128)}) custom-call(f32[3,6,8,128]{3,2,1,0:T(8,128)} %get-tuple-element.4.u_ref, f32[3,6,8,128]{3,2,1,0:T(8,128)} %get-tuple-element.5.v_ref), custom_call_target="tpu_custom_call" | custom-call | tf_op jit(solution)/shard_map/advance/pallas_call | solution.py:495
